TPU v7x, 32 devices: a whole 2x2x4 slice. The times are simulated.
32 devices in a mesh: kgrp: 8 (over y, x, core), img: 4 (over z).
Axes of the slice: x: 2, y: 2, z: 4, core: 2. Of those that a mesh axis runs over, the one named last changes fastest.
Arguments:
- vectors: float32 [2, 16, 1024], P(None, 'img', 'kgrp'), may hold values from -6 to 6
- conduction: bfloat16 [16, 2, 8, 4, 4096], P('kgrp', None, None, 'img'), may hold values from -6 to 6
- valence: bfloat16 [16, 2, 8, 4, 4096], P('kgrp', None, None, 'img'), may hold values from -6 to 6
- hole_point: int32 [1], replicated, may hold values from 0 to 16383
- kpoint_grid: int32 [3, 16], replicated, may hold values from 0 to 11
- image_cells: int32 [3, 512], replicated, may hold values from -6 to 6
Outputs:
- psi_real: float32 [16, 4, 4096, 512], P(None, 'img', 'kgrp')
- psi_imag: float32 [16, 4, 4096, 512], P(None, 'img', 'kgrp')
All inputs are finite; a program needn't handle non-finite values.
Results may differ from a plain program's by a relative error of at most 0.0043.
Values may be sent and summed in bfloat16 or wider, within the bound.
No kernel may reach another device: no remote copies, remote signals or barrier semaphores. Data moves between devices by JAX's collectives and lax.ppermute only.
A program may use at most 128 MiB of HBM per device.

v0:
```python
import jax
import jax.numpy as jnp
import numpy as np
from jax import lax
from jax.sharding import PartitionSpec as P

NV = 8
NC = 8


cosine_levels = np.cos(2.0 * np.pi * np.arange(12) / 12.0)
sine_levels = np.sin(2.0 * np.pi * np.arange(12) / 12.0)


def phase_table(kpoint_grid, image_cells):
    turn_count = kpoint_grid[0][:, None] * image_cells[0][None, :]
    turn_count = turn_count + kpoint_grid[1][:, None] * image_cells[1][None, :]
    turn_count = turn_count + kpoint_grid[2][:, None] * image_cells[2][None, :]
    turn_count = jnp.mod(turn_count, 12)
    cosine = jnp.zeros(turn_count.shape, jnp.float32)
    sine_part = jnp.zeros(turn_count.shape, jnp.float32)
    for level_index in range(12):
        matches = turn_count == level_index
        cosine = jnp.where(matches, jnp.float32(cosine_levels[level_index]), cosine)
        sine_part = jnp.where(matches, jnp.float32(sine_levels[level_index]), sine_part)
    upper_half = jnp.stack([cosine, sine_part], 1)
    lower_half = jnp.stack([-sine_part, cosine], 1)
    return jnp.stack([upper_half, lower_half], 0).astype(jnp.bfloat16)


def hole_weights(amplitudes, hole_values):
    norm_factor = (NV * NC) ** (-0.5)
    real_amplitude = amplitudes[0]
    imaginary_amplitude = amplitudes[1]
    real_hole = hole_values[:, 0]
    imaginary_hole = hole_values[:, 1]
    highest = lax.Precision.HIGHEST
    weight_real = jnp.einsum("skvc,kv->ksc", real_amplitude, real_hole, precision=highest)
    weight_real = weight_real + jnp.einsum(
        "skvc,kv->ksc", imaginary_amplitude, imaginary_hole, precision=highest
    )
    weight_imaginary = jnp.einsum("skvc,kv->ksc", imaginary_amplitude, real_hole, precision=highest)
    weight_imaginary = weight_imaginary - jnp.einsum(
        "skvc,kv->ksc", real_amplitude, imaginary_hole, precision=highest
    )
    return jnp.stack([weight_real * norm_factor, weight_imaginary * norm_factor], 1).astype(
        jnp.bfloat16
    )


def mixing(weights):
    weight_real = weights[:, 0]
    weight_imaginary = weights[:, 1]
    first_row = jnp.stack([weight_real, -weight_imaginary], 2)
    second_row = jnp.stack([weight_imaginary, weight_real], 2)
    return jnp.stack([first_row, second_row], 1)


def shards(vectors, conduction, valence, hole_point, kpoint_grid, image_cells):
    group_size = lax.axis_size("kgrp")
    local_k = conduction.shape[0]
    slab_width = conduction.shape[4]
    own_excitons = vectors.shape[1]
    blocks = vectors.shape[2] // group_size
    columns = vectors.reshape(2, own_excitons, group_size, blocks)
    owned_columns = lax.all_to_all(columns, "kgrp", split_axis=2, concat_axis=2, tiled=True)
    owned_columns = owned_columns.reshape(2, own_excitons, local_k, NV, NC)
    hole_offset = hole_point[0] % slab_width
    hole_slab = hole_point[0] // slab_width
    present = (lax.axis_index("img") == hole_slab).astype(jnp.float32)
    picked = (
        lax.dynamic_slice_in_dim(valence[:, :, :, 0, :], hole_offset, 1, 3)[..., 0].astype(
            jnp.float32
        )
        * present
    )
    hole_values = lax.psum(picked, "img")
    weights = lax.all_gather(hole_weights(owned_columns, hole_values), "img", axis=2, tiled=True)
    phases = phase_table(kpoint_grid, image_cells)
    products = jnp.einsum(
        "kasbc,kbcp->sakp",
        mixing(weights),
        conduction[:, :, :, 0, :],
        preferred_element_type=jnp.float32,
    ).astype(jnp.bfloat16)
    summed = jnp.einsum(
        "sakp,akbn->spbn",
        lax.all_to_all(products, "kgrp", split_axis=3, concat_axis=2, tiled=True),
        phases,
        preferred_element_type=jnp.float32,
    )
    normal_scale = (2 * kpoint_grid.shape[1]) ** (-0.5)
    summed = summed * normal_scale
    return (summed[:, None, :, 0, :], summed[:, None, :, 1, :])


def solution(mesh):
    placed = (
        P(None, "img", "kgrp"),
        P("kgrp", None, None, "img", None),
        P("kgrp", None, None, "img", None),
        P(),
        P(),
        P(),
    )
    return jax.shard_map(
        shards,
        mesh=mesh,
        in_specs=placed,
        out_specs=(P(None, "img", "kgrp", None), P(None, "img", "kgrp", None)),
        check_vma=False,
    )
```

profile of v0, /device:TPU:0, one launch (start us, length us, event | category | flops | bytes accessed | tf_op | source)
XLA Modules:
  0.0 113.5 jit_solution(17862852057084318996)
XLA Ops:
  0.6 0.8 reshape.639
  1.5 0.7 reshape.653
  2.2 5.2 %all-to-all-start = ((f32[8,1,128]{2,1,0:T(1,128)}), f32[8,1,128]{2,1,0:T(1,128)S(1)}, u32[]{:S(2)}, u32[]{:S(2)}) async-start(f32[8,1,128]{2,1,0:T(1,128)} %reshape.653), calls=%async_computation | async-start | bytes 8192 | tf_op jit(solution)/shard_map/all_to_all | solution.py:66
  7.4 0.8 fusion.27
  8.9 0.9 multiply_reduce_fusion
  9.7 11.9 %psum.7 = f32[2,2,8]{2,1,0:T(2,128)S(1)} all-reduce(f32[2,2,8]{2,1,0:T(2,128)S(1)} %multiply_reduce_fusion), channel_id=1, replica_groups=mesh['kgrp'=8,'img'=4] {'img'}, use_global_device_ids=true, to_apply=%region_0.1 | all-reduce | flops 32 | bytes 256 | tf_op jit(solution)/shard_map/psum | solution.py:77
  21.7 0.5 broadcast.739
  22.2 0.7 reduce.2
  23.0 0.2 fusion.13
  23.2 0.2 fusion.15
  23.4 0.2 fusion.9
  23.6 0.2 fusion.11
  23.8 13.2 %all_gather.3 = bf16[2,2,16,8]{3,1,0,2:T(2,128)(2,1)S(1)} all-gather(bf16[2,2,4,8]{3,1,0,2:T(2,128)(2,1)S(1)} %copy.34), channel_id=1, replica_groups=mesh['kgrp'=8,'img'=4] {'img'}, dimensions={2}, use_global_device_ids=true | all-gather | bytes 1280 | tf_op jit(solution)/shard_map/all_gather | solution.py:78
  37.3 0.3 fusion.1
  37.6 6.9 %copy.38 = bf16[16,2,2,4096]{0,1,2,3:T(2,128)(2,1)} copy(bf16[16,2,2,4096]{3,0,1,2:T(8,128)(2,1)S(1)} %fusion.1) | data formatting | bytes 1048576 | tf_op jit(solution)/shard_map/convert_element_type | solution.py:85
  44.5 6.5 %reshape.655 = bf16[8,2,16384]{2,1,0:T(2,128)(2,1)} reshape(bf16[4096,2,2,16]{3,2,1,0:T(2,128)(2,1)} %bitcast.101) | data formatting | bytes 1048576
  51.0 4.2 %all-to-all-start.1 = ((bf16[8,2,16384]{2,1,0:T(2,128)(2,1)}), bf16[8,2,16384]{2,1,0:T(2,128)(2,1)S(1)}, u32[]{:S(2)}, u32[]{:S(2)}) async-start(bf16[8,2,16384]{2,1,0:T(2,128)(2,1)} %reshape.655), calls=%async_computation.1 | async-start | bytes 1048576 | tf_op jit(solution)/shard_map/all_to_all | solution.py:88
  55.2 0.8 slice_bitcast_fusion.6
  56.1 8.8 %all-to-all-done.1 = bf16[8,2,16384]{2,1,0:T(2,128)(2,1)S(1)} async-done(((bf16[8,2,16384]{2,1,0:T(2,128)(2,1)}), bf16[8,2,16384]{2,1,0:T(2,128)(2,1)S(1)}, u32[]{:S(2)}, u32[]{:S(2)}) %all-to-all-start.1) | async-done | bytes 524320 | tf_op jit(solution)/shard_map/all_to_all | solution.py:88
  64.9 4.1 %reshape.656 = bf16[4096,2,2,16]{3,2,1,0:T(2,128)(2,1)} reshape(bf16[8,2,16384]{2,1,0:T(2,128)(2,1)S(1)} %all-to-all-done.1) | data formatting | bytes 1048576
  68.9 9.7 %copy.39 = bf16[16,2,2,8,512]{4,2,3,1,0:T(2,128)(2,1)S(1)} copy(bf16[16,2,2,8,512]{0,1,2,4,3:T(2,128)(2,1)} %bitcast.102) | data formatting | bytes 1048576 | tf_op jit(solution)/shard_map/all_to_all | solution.py:88
  78.7 0.2 reshape.648
  78.9 13.1 %bitcast_multiply_fusion = f32[16,512,2,512]{3,1,2,0:T(8,128)} fusion(bf16[16,2,16,512,1]{3,2,1,0,4:T(8,128)(2,1)S(1)} %reshape.648, bf16[1,16,2,512]{3,1,0,2:T(8,128)(2,1)S(1)} %get-tuple-element.15, bf16[1,16,2,512]{3,1,0,2:T(8,128)(2,1)S(1)} %get-tuple-element.14), kind=kOutput, calls=%fused_computation | convolution fusion | flops 545390592 | bytes 34144256 | tf_op jit(solution)/shard_map/sakp,akbn->spbn/dot_general | solution.py:86
  91.9 21.5 %slice_bitcast_fusion = (f32[16,1,512,512]{3,2,1,0:T(8,128)}, f32[16,1,512,512]{3,2,1,0:T(8,128)}) fusion(f32[16,512,2,512]{3,1,2,0:T(8,128)} %bitcast_multiply_fusion), kind=kLoop, calls=%fused_computation.1 | loop fusion | bytes 67108864
  (22 shorter events, 0.7 us)
Async XLA Ops:
  0.6 36.6 %copy-start = (bf16[2,2,8,1,4096]{4,2,3,1,0:T(8,128)(2,1)S(1)}, bf16[2,2,8,1,4096]{4,2,3,1,0:T(8,128)(2,1)}, u32[]{:S(2)}) copy-start(bf16[2,2,8,1,4096]{4,2,3,1,0:T(8,128)(2,1)} %param.7) | copy-start | bytes 786436
  2.2 19.5 %all-to-all-start = ((f32[8,1,128]{2,1,0:T(1,128)}), f32[8,1,128]{2,1,0:T(1,128)S(1)}, u32[]{:S(2)}, u32[]{:S(2)}) async-start(f32[8,1,128]{2,1,0:T(1,128)} %reshape.653), calls=%async_computation | async-start | bytes 8192 | tf_op jit(solution)/shard_map/all_to_all | solution.py:66
  51.0 13.9 %all-to-all-start.1 = ((bf16[8,2,16384]{2,1,0:T(2,128)(2,1)}), bf16[8,2,16384]{2,1,0:T(2,128)(2,1)S(1)}, u32[]{:S(2)}, u32[]{:S(2)}) async-start(bf16[8,2,16384]{2,1,0:T(2,128)(2,1)} %reshape.655), calls=%async_computation.1 | async-start | bytes 1048576 | tf_op jit(solution)/shard_map/all_to_all | solution.py:88
  91.9 21.5 %copy-start.1 = (bf16[2,2,8,1,4096]{4,2,3,1,0:T(8,128)(2,1)S(1)}, bf16[2,2,8,1,4096]{4,2,3,1,0:T(8,128)(2,1)}, u32[]{:S(2)}) copy-start(bf16[2,2,8,1,4096]{4,2,3,1,0:T(8,128)(2,1)} %param.7) | copy-start | bytes 786436
where the time goes:
time: 114 us; the launch traced here: 113 us
  local copies, waits for them, and re-layouts  53 us (46%)
  blocking collectives  25.2 us (22%)
  matrix products  14.1 us (12%)
  starting transfers between devices  9.4 us (8%)
  waiting for transfers between devices  8.76 us (8%)
  other arithmetic  1.71 us (2%)
  between operations  1.44 us (1%)
    unnamed x11, local copies, waits for them, and re-layouts  33 us
    all_gather x1, blocking collectives, shards(): lax.all_gather(hole_weights(owned_columns, hole_values), 'img', axis=2, t...  13.2 us
    dot_general x1, matrix products, shards(): jnp.einsum('sakp,akbn->spbn', lax.all_to_all(products, 'kgrp', split_axis...  13.1 us
    psum x1, blocking collectives, shards(): hole_values = lax.psum(picked, 'img')  11.9 us
    all_to_all x2, local copies, waits for them, and re-layouts, shards(): lax.all_to_all(products, 'kgrp', split_axis=3, concat_axis=2, tiled=True)  9.93 us
    all_to_all x1, waiting for transfers between devices, shards(): lax.all_to_all(products, 'kgrp', split_axis=3, concat_axis=2, tiled=True)  8.76 us
    convert_element_type x1, local copies, waits for them, and re-layouts, shards(): products = jnp.einsum('kasbc,kbcp->sakp', mixing(weights), conduction[:,...  6.9 us
    all_to_all x1, starting transfers between devices, shards(): lax.all_to_all(columns, 'kgrp', split_axis=2, concat_axis=2, tiled=True)  5.2 us
  transfers between devices with their start and end apart: 2, of which 1 were waited for; matrix products, arithmetic and copies ran while one was open for 2% of the time, Pallas kernels for 0%

commit v1 on v0

--- a/solution.py
+++ b/solution.py
@@ -1,15 +1,306 @@
+import functools
+
 import jax
 import jax.numpy as jnp
 import numpy as np
 from jax import lax
+from jax.experimental import pallas as pl
+from jax.experimental.pallas import tpu as pltpu
 from jax.sharding import PartitionSpec as P
+
 
 NV = 8
 NC = 8
-
+LANES = 128
+MIB = 1 << 20
 
 cosine_levels = np.cos(2.0 * np.pi * np.arange(12) / 12.0)
 sine_levels = np.sin(2.0 * np.pi * np.arange(12) / 12.0)
+
+VMEM = pltpu.MemorySpace.VMEM
+SMEM = pltpu.MemorySpace.SMEM
+ANY = pl.ANY
+
+
+def iota(shape, axis):
+    return lax.broadcasted_iota(jnp.int32, shape, axis)
+
+
+def pack_kernel(slab_width, hole_ref, vector_ref, valence_ref, out_ref):
+    local_k = valence_ref.shape[0]
+    own = vector_ref.shape[1]
+    width = vector_ref.shape[2]
+    hole = hole_ref[0]
+    present = hole // slab_width == lax.axis_index("img")
+    lane = jnp.where(present, lax.rem(lax.rem(hole, slab_width), LANES), -1)
+    keep = iota((NV, LANES), 1) == lane
+    target = iota((NV, width), 1) // NC - iota((NV, width), 0)
+    rows = []
+    for part in range(2):
+        spread = jnp.zeros((NV, width), jnp.float32)
+        for q in range(local_k):
+            values = jnp.where(keep, valence_ref[q, part].astype(jnp.float32), 0.0)
+            column = jnp.sum(values, axis=1, keepdims=True)
+            spread = jnp.where(target == q * NV, column, spread)
+        rows.append(jnp.sum(spread, axis=0, keepdims=True))
+    pad = out_ref.shape[1] - 2 * own - 2
+    block = jnp.concatenate(
+        [vector_ref[0], vector_ref[1]] + rows + [jnp.zeros((pad, width), jnp.float32)], 0
+    )
+    out_ref[...] = jnp.broadcast_to(block[None], out_ref.shape)
+
+
+def pack(vectors, valence, hole_point, devices):
+    own, width = vectors.shape[1:]
+    slab_width = valence.shape[3]
+    local_k = valence.shape[0]
+    rows = -(-(2 * own + 2) // 8) * 8
+    return pl.pallas_call(
+        functools.partial(pack_kernel, slab_width),
+        out_shape=jax.ShapeDtypeStruct((devices, rows, width), jnp.float32),
+        grid_spec=pltpu.PrefetchScalarGridSpec(
+            num_scalar_prefetch=1,
+            grid=(1,),
+            in_specs=[
+                pl.BlockSpec((2, own, width), lambda i, h: (0, 0, 0)),
+                pl.BlockSpec(
+                    (local_k, 2, NV, LANES),
+                    lambda i, h: (0, 0, 0, lax.rem(h[0], slab_width) // LANES),
+                ),
+            ],
+            out_specs=pl.BlockSpec((devices, rows, width), lambda i, h: (0, 0, 0)),
+        ),
+        compiler_params=pltpu.CompilerParams(vmem_limit_bytes=4 * MIB),
+        name="pack",
+    )(hole_point, vectors, valence)
+
+
+def cut_kernel(cond_ref, *outs):
+    me = lax.axis_index("kgrp")
+    width = outs[0].shape[-1]
+    for step, out_ref in enumerate(outs):
+        start = pl.multiple_of(jnp.bitwise_xor(me, step) * width, width)
+        out_ref[...] = cond_ref[:, :, :, pl.ds(start, width)]
+
+
+def cut(cond, group):
+    piece = cond.shape[:3] + (cond.shape[3] // group,)
+    return pl.pallas_call(
+        cut_kernel,
+        out_shape=[jax.ShapeDtypeStruct(piece, cond.dtype)] * group,
+        in_specs=[pl.BlockSpec(memory_space=VMEM)],
+        out_specs=[pl.BlockSpec(memory_space=VMEM)] * group,
+        compiler_params=pltpu.CompilerParams(vmem_limit_bytes=4 * MIB),
+        name="cut",
+    )(cond)
+
+
+def blocks_of(local_k, width):
+    chunks = [(q, j) for q in range(local_k) for j in range(width // LANES)]
+    return [chunks[i:i + 2] for i in range(0, len(chunks), 2)]
+
+
+def stage_kernel(blocks, grid_ref, cells_ref, *refs):
+    pieces, (points_ref, phase_ref, held) = refs[:-3], refs[-3:]
+    me = lax.axis_index("kgrp")
+    local_k = pieces[0].shape[0]
+    for step, piece in enumerate(pieces):
+        held[jnp.bitwise_xor(me, step)] = piece[...].reshape(held.shape[1:])
+    images = cells_ref.shape[1]
+    places = phase_ref.shape[1]
+    for index, block in enumerate(blocks):
+        parts = []
+        owners = []
+        for q, j in block:
+            owners += [(8 * j + i) * local_k + q for i in range(8)]
+            for i in range(8):
+                parts.append(held[8 * j + i, q].astype(jnp.float32))
+        points_ref[index] = jnp.concatenate(parts, 0).T.astype(jnp.bfloat16)
+        row = iota((16, images), 0)
+        turn = jnp.zeros((16, images), jnp.int32)
+        for axis in range(3):
+            column = jnp.zeros((16, images), jnp.int32)
+            for place, k in enumerate(owners):
+                column = jnp.where(row == place, grid_ref[axis, k], column)
+            turn = turn + column * cells_ref[axis:axis + 1, :]
+        count = turn.astype(jnp.float32)
+        count = count - 12.0 * jnp.floor((count + 0.5) / 12.0)
+        cosine = jnp.zeros((16, images), jnp.float32)
+        sine = jnp.zeros((16, images), jnp.float32)
+        for level in range(12):
+            match = count == float(level)
+            cosine = jnp.where(match, float(cosine_levels[level]), cosine)
+            sine = jnp.where(match, float(sine_levels[level]), sine)
+        upper = jnp.concatenate([cosine, sine], 1)
+        lower = jnp.concatenate([-sine, cosine], 1)
+        table = jnp.concatenate([upper, lower], 0).astype(jnp.bfloat16)
+        phase_ref[index] = jnp.zeros(phase_ref.shape[1:], jnp.bfloat16)
+        for place in range(places):
+            phase_ref[index, place, 32 * place:32 * place + 32, :] = table
+
+
+def stage(kpoint_grid, image_cells, pieces, width):
+    group = len(pieces)
+    local_k, _, _, points = pieces[0].shape
+    images = image_cells.shape[1]
+    blocks = blocks_of(local_k, width)
+    return pl.pallas_call(
+        functools.partial(stage_kernel, blocks),
+        out_shape=[
+            jax.ShapeDtypeStruct((len(blocks), points, 256), jnp.bfloat16),
+            jax.ShapeDtypeStruct((len(blocks), 4, LANES, 2 * images), jnp.bfloat16),
+        ],
+        in_specs=[pl.BlockSpec(memory_space=SMEM)]
+        + [pl.BlockSpec(memory_space=VMEM)] * (1 + group),
+        out_specs=[pl.BlockSpec(memory_space=VMEM)] * 2,
+        scratch_shapes=[pltpu.VMEM((group, local_k, 2 * NC, points), jnp.bfloat16)],
+        compiler_params=pltpu.CompilerParams(vmem_limit_bytes=12 * MIB),
+        name="stage",
+    )(kpoint_grid, image_cells, *pieces)
+
+
+def swap_blocks(x, block):
+    count, width = x.shape
+    row = iota(x.shape, 0)
+    column = iota(x.shape, 1) // block
+    step = 1
+    while step < count:
+        low_row = (row & step) == 0
+        low_column = (column & step) == 0
+        down = pltpu.roll(pltpu.roll(x, count - step, 0), step * block, 1)
+        up = pltpu.roll(pltpu.roll(x, step, 0), width - step * block, 1)
+        x = jnp.where(low_row == low_column, x, jnp.where(low_row, down, up))
+        step *= 2
+    return x
+
+
+def psi_kernel(blocks, own, img, all_ref, points_ref, phase_ref, real_ref, imag_ref, table, product, out, sems):
+    devices, _, width = all_ref.shape
+    group = devices // img
+    excitons = own * img
+    block = width // group
+    per_k = NV * NC // block
+    points = points_ref.shape[1]
+    images = phase_ref.shape[3] // 2
+    norm_factor = (NV * NC) ** (-0.5)
+    scale = (32 * len(blocks)) ** (-0.5)
+
+    hole_real = []
+    hole_imag = []
+    for i in range(group):
+        total = all_ref[i * img, 2 * own:, :]
+        for z in range(1, img):
+            total = total + all_ref[i * img + z, 2 * own:, :]
+        hole_real.append(total[0:1])
+        hole_imag.append(total[1:2])
+    hole_real = swap_blocks(jnp.concatenate(hole_real, 0), block)
+    hole_imag = swap_blocks(jnp.concatenate(hole_imag, 0), block)
+    shape = (2 * own, width)
+    sign = jnp.where(iota(shape, 0) < own, 1.0, -1.0)
+    low = (iota(shape, 1) // NC) % 2 == 0
+    coupled = {}
+    for q in range(width // (NV * NC)):
+        for z in range(img):
+            total = jnp.zeros(shape, jnp.float32)
+            for d in range(q * per_k, (q + 1) * per_k):
+                x = all_ref[d * img + z, :2 * own, :]
+                turned = pltpu.roll(x, own, 0)
+                total = total + x * hole_real[d:d + 1] + sign * turned * hole_imag[d:d + 1]
+            other = jnp.where(low, pltpu.roll(total, width - NC, 1), pltpu.roll(total, NC, 1))
+            total = (total + other) * norm_factor
+            total = jnp.where(low, total, -sign * pltpu.roll(total, own, 0))
+            coupled[q, z] = total
+    place = iota((16, LANES), 0)
+    column = iota((16, LANES), 1) // (2 * NC)
+    for index, pair in enumerate(blocks):
+        for z in range(img):
+            for e in range(own):
+                s = z * own + e
+                for part in range(2):
+                    for half, (q, j) in enumerate(pair):
+                        line = coupled[q, z][part * own + e:part * own + e + 1, j * LANES:(j + 1) * LANES]
+                        spread = jnp.where(place == column + 8 * half, line, 0.0)
+                        table[
+                            index,
+                            32 * s + 16 * part:32 * s + 16 * part + 16,
+                            half * LANES:(half + 1) * LANES,
+                        ] = spread.astype(jnp.bfloat16)
+        for g in range(excitons // 4):
+            product[index, g] = lax.dot_general(
+                points_ref[index],
+                table[index, g * LANES:(g + 1) * LANES, :],
+                (((1,), (1,)), ((), ())),
+                preferred_element_type=jnp.float32,
+            ).astype(jnp.bfloat16)
+
+    slots, _, rows, _ = out.shape
+    cuts = points // rows
+    steps = excitons * cuts
+
+    def copies(step, slot):
+        s = step // cuts
+        start = lax.rem(step, cuts) * rows
+        return [
+            pltpu.make_async_copy(
+                out.at[slot, part],
+                ref.at[s, 0, pl.ds(start, rows), :],
+                sems.at[slot, part],
+            )
+            for part, ref in enumerate((real_ref, imag_ref))
+        ]
+
+    @pl.loop(0, steps)
+    def _(step):
+        slot = lax.rem(step, slots)
+
+        @pl.when(step >= slots)
+        def _():
+            for copy in copies(step - slots, slot):
+                copy.wait()
+
+        s = step // cuts
+        start = pl.multiple_of(lax.rem(step, cuts) * rows, rows)
+        for part in range(2):
+            total = None
+            for index in range(len(blocks)):
+                term = jnp.dot(
+                    product[index, s // 4, pl.ds(start, rows), :],
+                    phase_ref[index, lax.rem(s, 4), :, part * images:(part + 1) * images],
+                    preferred_element_type=jnp.float32,
+                )
+                total = term if total is None else total + term
+            out[slot, part] = total * scale
+        for copy in copies(step, slot):
+            copy.start()
+
+    for step in range(steps - slots, steps):
+        for copy in copies(step, step % slots):
+            copy.wait()
+
+
+def psi(gathered, points, phases, own, img):
+    width = gathered.shape[2]
+    local_k = width // (NV * NC)
+    blocks = blocks_of(local_k, width)
+    excitons = own * img
+    count = points.shape[1]
+    images = phases.shape[3] // 2
+    rows = min(count, 512)
+    shape = jax.ShapeDtypeStruct((excitons, 1, count, images), jnp.float32)
+    return pl.pallas_call(
+        functools.partial(psi_kernel, blocks, own, img),
+        out_shape=[shape, shape],
+        in_specs=[pl.BlockSpec(memory_space=VMEM)] * 3,
+        out_specs=[pl.BlockSpec(memory_space=ANY)] * 2,
+        scratch_shapes=[
+            pltpu.VMEM((len(blocks), 32 * excitons, 256), jnp.bfloat16),
+            pltpu.VMEM((len(blocks), excitons // 4, count, LANES), jnp.bfloat16),
+            pltpu.VMEM((4, 2, rows, images), jnp.float32),
+            pltpu.SemaphoreType.DMA((4, 2)),
+        ],
+        compiler_params=pltpu.CompilerParams(vmem_limit_bytes=24 * MIB),
+        name="psi",
+    )(gathered, points, phases)
 
 
 def phase_table(kpoint_grid, image_cells):
@@ -56,7 +347,7 @@
     return jnp.stack([first_row, second_row], 1)
 
 
-def shards(vectors, conduction, valence, hole_point, kpoint_grid, image_cells):
+def general_shards(vectors, conduction, valence, hole_point, kpoint_grid, image_cells):
     group_size = lax.axis_size("kgrp")
     local_k = conduction.shape[0]
     slab_width = conduction.shape[4]
@@ -94,6 +385,25 @@
     return (summed[:, None, :, 0, :], summed[:, None, :, 1, :])
 
 
+def shards(vectors, conduction, valence, hole_point, kpoint_grid, image_cells):
+    group = lax.axis_size("kgrp")
+    img = lax.axis_size("img")
+    own = vectors.shape[1]
+    width = vectors.shape[2]
+    points = conduction.shape[4] // group
+    if width // group != 2 * NC or width % LANES or points % LANES or group & (group - 1) or own != 4:
+        return general_shards(vectors, conduction, valence, hole_point, kpoint_grid, image_cells)
+    packed = pack(vectors, valence[:, :, :, 0, :], hole_point, group * img)
+    gathered = lax.all_to_all(packed, ("kgrp", "img"), 0, 0, tiled=True)
+    pieces = list(cut(conduction[:, :, :, 0, :], group))
+    for step in range(1, group):
+        pairs = [(i, i ^ step) for i in range(group)]
+        pieces[step] = lax.ppermute(pieces[step], "kgrp", pairs)
+    points, phases = stage(kpoint_grid, image_cells, pieces, width)
+    real, imag = psi(gathered, points, phases, own, img)
+    return real, imag
+
+
 def solution(mesh):
     placed = (
         P(None, "img", "kgrp"),

time: 114 us -> 37.4 us (0.33)
  local copies, waits for them, and re-layouts: 53 us -> 3.95 us
  blocking collectives: 25.2 us -> 0 us
  matrix products: 14.1 us -> 0 us
  Pallas kernels: 0 us -> 13.8 us
  waiting for transfers between devices: 8.76 us -> 4.23 us
  starting transfers between devices: 9.4 us -> 13.7 us
  other arithmetic: 1.71 us -> 0 us
    unnamed x11 -> x10, local copies, waits for them, and re-layouts: 33 us -> 3.95 us
    dot_general x6 -> x0, matrix products: 14.1 us -> none  [the longest x1 13.1 us: shards(): jnp.einsum('sakp,akbn->spbn', lax.all_to_all(products, 'kgrp', split_axis...]
    pallas_call x0 -> x4, Pallas kernels: none -> 13.8 us  [the longest x1 12.1 us: psi(): pl.pallas_call(functools.partial(psi_kernel, blocks, own, img), out_shape...]
    all_gather x1 -> x0, blocking collectives: 13.2 us -> none  [shards(): lax.all_gather(hole_weights(owned_columns, hole_values), 'img', axis=2, t...]
    psum x1 -> x0, blocking collectives: 11.9 us -> none  [shards(): hole_values = lax.psum(picked, 'img')]
    all_to_all x3 -> x0, local copies, waits for them, and re-layouts: 10.4 us -> none  [the longest x2 9.93 us: shards(): lax.all_to_all(products, 'kgrp', split_axis=3, concat_axis=2, tiled=True)]
    all_to_all x2 -> x1, waiting for transfers between devices: 8.76 us -> 0.01 us  [shards(): gathered = lax.all_to_all(packed, ('kgrp', 'img'), 0, 0, tiled=True)]
    convert_element_type x1 -> x0, local copies, waits for them, and re-layouts: 6.9 us -> none  [shards(): products = jnp.einsum('kasbc,kbcp->sakp', mixing(weights), conduction[:,...]
  transfers between devices with their start and end apart: 2 -> 8, of which waited for: 1 -> 3; matrix products, arithmetic and copies ran while one was open for 2% -> 0% of each run, Pallas kernels for 0% -> 2%
where the time goes in v1:
time: 37.4 us; the launch traced here: 37 us
  Pallas kernels  13.8 us (37%)
  starting transfers between devices  13.7 us (37%)
  waiting for transfers between devices  4.23 us (11%)
  local copies, waits for them, and re-layouts  3.95 us (11%)
  between operations  1.33 us (4%)
    pallas_call x1, Pallas kernels, psi(): pl.pallas_call(functools.partial(psi_kernel, blocks, own, img), out_shape...  12.1 us
    all_to_all x1, starting transfers between devices, shards(): gathered = lax.all_to_all(packed, ('kgrp', 'img'), 0, 0, tiled=True)  7.33 us
    ppermute x7, starting transfers between devices, shards(): pieces[step] = lax.ppermute(pieces[step], 'kgrp', pairs)  6.41 us
    ppermute x7, waiting for transfers between devices, shards(): pieces[step] = lax.ppermute(pieces[step], 'kgrp', pairs)  4.23 us
    unnamed x10, local copies, waits for them, and re-layouts  3.95 us
    pallas_call x1, Pallas kernels, pack(): pl.pallas_call(functools.partial(pack_kernel, slab_width), out_shape=jax....  0.82 us
    pallas_call x1, Pallas kernels, stage(): pl.pallas_call(functools.partial(stage_kernel, blocks), out_shape=[jax.Sh...  0.81 us
  transfers between devices with their start and end apart: 8, of which 3 were waited for; matrix products, arithmetic and copies ran while one was open for 0% of the time, Pallas kernels for 2%

profile of v1, /device:TPU:0, one launch (start us, length us, event | category | flops | bytes accessed | tf_op | source)
XLA Modules:
  0.0 37.0 jit_solution(8398525863398127770)
XLA Ops:
  1.3 0.9 %copy-done = bf16[2,2,8,1,4096]{4,2,3,1,0:T(8,128)(2,1)S(1)} copy-done((bf16[2,2,8,1,4096]{4,2,3,1,0:T(8,128)(2,1)S(1)}, bf16[2,2,8,1,4096]{4,2,3,1,0:T(8,128)(2,1)}, u32[]{:S(2)}) %copy-start) | copy-done | bytes 262168
  2.2 0.7 %copy-done.3 = f32[2,4,128]{2,1,0:T(4,128)S(1)} copy-done((f32[2,4,128]{2,1,0:T(4,128)S(1)}, f32[2,4,128]{2,1,0:T(4,128)}, u32[]{:S(2)}) %copy-start.3) | copy-done | bytes 4120
  2.9 0.8 %pack.1 = f32[32,16,128]{2,1,0:T(8,128)} custom-call(s32[1]{0:T(128)S(6)} %copy.8.hole_ref, f32[2,4,128]{2,1,0:T(4,128)S(1)} %copy-done.3, bf16[2,2,8,4096]{3,2,1,0:T(8,128)(2,1)S(1)} %bitcast.2), custom_call_target="tpu_custom_call" | custom-call | tf_op jit(solution)/shard_map/pack/pallas_call | solution.py:58
  3.7 7.3 %all-to-all-start = ((f32[32,16,128]{2,1,0:T(8,128)}), f32[32,16,128]{2,1,0:T(8,128)S(1)}, u32[]{:S(2)}, u32[]{:S(2)}) async-start(f32[32,16,128]{2,1,0:T(8,128)} %pack.1), calls=%async_computation | async-start | bytes 524288 | tf_op jit(solution)/shard_map/all_to_all | solution.py:397
  11.1 0.0 copy-start.1
  11.1 0.9 %copy-done.1 = bf16[2,2,8,1,4096]{4,2,3,1,0:T(8,128)(2,1)S(1)} copy-done((bf16[2,2,8,1,4096]{4,2,3,1,0:T(8,128)(2,1)S(1)}, bf16[2,2,8,1,4096]{4,2,3,1,0:T(8,128)(2,1)}, u32[]{:S(2)}) %copy-start.1) | copy-done | bytes 262168
  12.0 0.3 collective-permute-start
  12.4 1.6 %collective-permute-start.1 = (bf16[2,2,8,512]{3,2,1,0:T(8,128)(2,1)S(1)}, bf16[2,2,8,512]{3,2,1,0:T(8,128)(2,1)S(1)}, u32[]{:S(2)}, u32[]{:S(2)}) collective-permute-start(bf16[2,2,8,512]{3,2,1,0:T(8,128)(2,1)S(1)} %get-tuple-element.14), channel_id=1, source_target_pairs={{0,8},{4,12},{8,0},{12,4},{16,24},{20,28},{24,16},{28,20},{1,9},{5... | collective-permute-start | bytes 98312 | tf_op jit(solution)/shard_map/ppermute | solution.py:401
  14.0 0.0 collective-permute-start.2
  14.0 1.7 %collective-permute-start.3 = (bf16[2,2,8,512]{3,2,1,0:T(8,128)(2,1)S(1)}, bf16[2,2,8,512]{3,2,1,0:T(8,128)(2,1)S(1)}, u32[]{:S(2)}, u32[]{:S(2)}) collective-permute-start(bf16[2,2,8,512]{3,2,1,0:T(8,128)(2,1)S(1)} %get-tuple-element.16), channel_id=1, source_target_pairs={{0,16},{4,20},{8,24},{12,28},{16,0},{20,4},{24,8},{28,12},{1,17},{... | collective-permute-start | bytes 98312 | tf_op jit(solution)/shard_map/ppermute | solution.py:401
  15.7 0.1 collective-permute-start.4
  15.8 0.0 collective-permute-done.refs_1_
  15.9 2.5 %collective-permute-start.5 = (bf16[2,2,8,512]{3,2,1,0:T(8,128)(2,1)S(1)}, bf16[2,2,8,512]{3,2,1,0:T(8,128)(2,1)S(1)}, u32[]{:S(2)}, u32[]{:S(2)}) collective-permute-start(bf16[2,2,8,512]{3,2,1,0:T(8,128)(2,1)S(1)} %get-tuple-element.18), channel_id=1, source_target_pairs={{0,24},{4,28},{8,16},{12,20},{16,8},{20,12},{24,0},{28,4},{1,25},{... | collective-permute-start | bytes 98312 | tf_op jit(solution)/shard_map/ppermute | solution.py:401
  18.4 0.0 collective-permute-done.1.refs_2_
  18.4 0.1 collective-permute-start.6
  18.5 0.0 collective-permute-done.2.refs_3_
  18.5 0.0 collective-permute-done.3.refs_4_
  18.5 0.8 %collective-permute-done.4.refs_5_ = bf16[2,2,8,512]{3,2,1,0:T(8,128)(2,1)S(1)} collective-permute-done((bf16[2,2,8,512]{3,2,1,0:T(8,128)(2,1)S(1)}, bf16[2,2,8,512]{3,2,1,0:T(8,128)(2,1)S(1)}, u32[]{:S(2)}, u32[]{:S(2)}) %collective-permute-start.4) | collective-permute-done | bytes 32800 | tf_op jit(solution)/shard_map/ppermute | solution.py:401
  19.3 1.4 %collective-permute-done.5.refs_6_ = bf16[2,2,8,512]{3,2,1,0:T(8,128)(2,1)S(1)} collective-permute-done((bf16[2,2,8,512]{3,2,1,0:T(8,128)(2,1)S(1)}, bf16[2,2,8,512]{3,2,1,0:T(8,128)(2,1)S(1)}, u32[]{:S(2)}, u32[]{:S(2)}) %collective-permute-start.5) | collective-permute-done | bytes 32800 | tf_op jit(solution)/shard_map/ppermute | solution.py:401
  20.8 1.9 %collective-permute-done.6.refs_7_ = bf16[2,2,8,512]{3,2,1,0:T(8,128)(2,1)S(1)} collective-permute-done((bf16[2,2,8,512]{3,2,1,0:T(8,128)(2,1)S(1)}, bf16[2,2,8,512]{3,2,1,0:T(8,128)(2,1)S(1)}, u32[]{:S(2)}, u32[]{:S(2)}) %collective-permute-start.6) | collective-permute-done | bytes 32800 | tf_op jit(solution)/shard_map/ppermute | solution.py:401
  22.7 0.7 %copy-done.2 = s32[3,512]{1,0:T(4,128)S(1)} copy-done((s32[3,512]{1,0:T(4,128)S(1)}, s32[3,512]{1,0:T(4,128)}, u32[]{:S(2)}) %copy-start.2) | copy-done | bytes 6168
  23.4 0.7 %copy-done.4 = s32[3,16]{1,0:T(4,128)S(1)} copy-done((s32[3,16]{1,0:T(4,128)S(1)}, s32[3,16]{1,0:T(4,128)}, u32[]{:S(2)}) %copy-start.4) | copy-done | bytes 216
  24.1 0.8 %stage.1 = (bf16[1,512,256]{2,1,0:T(8,128)(2,1)S(1)}, bf16[1,4,128,1024]{3,2,1,0:T(8,128)(2,1)S(1)}) custom-call(s32[3,16]{1,0:T(4,128)S(1)} %copy-done.4, s32[3,512]{1,0:T(4,128)S(1)} %copy-done.2, bf16[2,2,8,512]{3,2,1,0:T(8,128)(2,1)S(1)} %get-tuple-element.12.refs_0_, bf16[2,2,8,512]{3,2,1,0:T(8,128)(2,1)S(1)} %collective-permute-done.refs_1_, ...), custom_call_target="tpu_custom_call" | custom-call | tf_op jit(solution)/shard_map/stage/pallas_call | solution.py:147
  24.9 12.1 %psi.1 = (f32[16,1,512,512]{3,2,1,0:T(8,128)}, f32[16,1,512,512]{3,2,1,0:T(8,128)}) custom-call(f32[32,16,128]{2,1,0:T(8,128)S(1)} %all-to-all-done.all_ref, bf16[1,512,256]{2,1,0:T(8,128)(2,1)S(1)} %get-tuple-element.20.points_ref, bf16[1,4,128,1024]{3,2,1,0:T(8,128)(2,1)S(1)} %get-tuple-element.21.phase_ref), custom_call_target="tpu_custom_call" | custom-call | tf_op jit(solution)/shard_map/psi/pallas_call | solution.py:290
  (6 shorter events, 0.0 us)
Async XLA Ops:
  1.3 1.0 %copy-start = (bf16[2,2,8,1,4096]{4,2,3,1,0:T(8,128)(2,1)S(1)}, bf16[2,2,8,1,4096]{4,2,3,1,0:T(8,128)(2,1)}, u32[]{:S(2)}) copy-start(bf16[2,2,8,1,4096]{4,2,3,1,0:T(8,128)(2,1)} %param.8) | copy-start | bytes 786436
  2.2 0.7 %copy-start.3 = (f32[2,4,128]{2,1,0:T(4,128)S(1)}, f32[2,4,128]{2,1,0:T(4,128)}, u32[]{:S(2)}) copy-start(f32[2,4,128]{2,1,0:T(4,128)} %vector_ref.1) | copy-start | bytes 12292
  3.7 21.2 %all-to-all-start = ((f32[32,16,128]{2,1,0:T(8,128)}), f32[32,16,128]{2,1,0:T(8,128)S(1)}, u32[]{:S(2)}, u32[]{:S(2)}) async-start(f32[32,16,128]{2,1,0:T(8,128)} %pack.1), calls=%async_computation | async-start | bytes 524288 | tf_op jit(solution)/shard_map/all_to_all | solution.py:397
  11.1 1.0 %copy-start.1 = (bf16[2,2,8,1,4096]{4,2,3,1,0:T(8,128)(2,1)S(1)}, bf16[2,2,8,1,4096]{4,2,3,1,0:T(8,128)(2,1)}, u32[]{:S(2)}) copy-start(bf16[2,2,8,1,4096]{4,2,3,1,0:T(8,128)(2,1)} %param.7) | copy-start | bytes 786436
  12.0 3.8 %collective-permute-start = (bf16[2,2,8,512]{3,2,1,0:T(8,128)(2,1)S(1)}, bf16[2,2,8,512]{3,2,1,0:T(8,128)(2,1)S(1)}, u32[]{:S(2)}, u32[]{:S(2)}) collective-permute-start(bf16[2,2,8,512]{3,2,1,0:T(8,128)(2,1)S(1)} %get-tuple-element.13), channel_id=1, source_target_pairs={{0,4},{4,0},{8,12},{12,8},{16,20},{20,16},{24,28},{28,24},{1,5},{5... | collective-permute-start | bytes 98312 | tf_op jit(solution)/shard_map/ppermute | solution.py:401
  12.4 6.0 %collective-permute-start.1 = (bf16[2,2,8,512]{3,2,1,0:T(8,128)(2,1)S(1)}, bf16[2,2,8,512]{3,2,1,0:T(8,128)(2,1)S(1)}, u32[]{:S(2)}, u32[]{:S(2)}) collective-permute-start(bf16[2,2,8,512]{3,2,1,0:T(8,128)(2,1)S(1)} %get-tuple-element.14), channel_id=1, source_target_pairs={{0,8},{4,12},{8,0},{12,4},{16,24},{20,28},{24,16},{28,20},{1,9},{5... | collective-permute-start | bytes 98312 | tf_op jit(solution)/shard_map/ppermute | solution.py:401
  14.0 4.5 %collective-permute-start.2 = (bf16[2,2,8,512]{3,2,1,0:T(8,128)(2,1)S(1)}, bf16[2,2,8,512]{3,2,1,0:T(8,128)(2,1)S(1)}, u32[]{:S(2)}, u32[]{:S(2)}) collective-permute-start(bf16[2,2,8,512]{3,2,1,0:T(8,128)(2,1)S(1)} %get-tuple-element.15), channel_id=1, source_target_pairs={{0,12},{4,8},{8,4},{12,0},{16,28},{20,24},{24,20},{28,16},{1,13},{... | collective-permute-start | bytes 98312 | tf_op jit(solution)/shard_map/ppermute | solution.py:401
  14.0 4.5 %collective-permute-start.3 = (bf16[2,2,8,512]{3,2,1,0:T(8,128)(2,1)S(1)}, bf16[2,2,8,512]{3,2,1,0:T(8,128)(2,1)S(1)}, u32[]{:S(2)}, u32[]{:S(2)}) collective-permute-start(bf16[2,2,8,512]{3,2,1,0:T(8,128)(2,1)S(1)} %get-tuple-element.16), channel_id=1, source_target_pairs={{0,16},{4,20},{8,24},{12,28},{16,0},{20,4},{24,8},{28,12},{1,17},{... | collective-permute-start | bytes 98312 | tf_op jit(solution)/shard_map/ppermute | solution.py:401
  15.7 3.6 %collective-permute-start.4 = (bf16[2,2,8,512]{3,2,1,0:T(8,128)(2,1)S(1)}, bf16[2,2,8,512]{3,2,1,0:T(8,128)(2,1)S(1)}, u32[]{:S(2)}, u32[]{:S(2)}) collective-permute-start(bf16[2,2,8,512]{3,2,1,0:T(8,128)(2,1)S(1)} %get-tuple-element.17), channel_id=1, source_target_pairs={{0,20},{4,16},{8,28},{12,24},{16,4},{20,0},{24,12},{28,8},{1,21},{... | collective-permute-start | bytes 98312 | tf_op jit(solution)/shard_map/ppermute | solution.py:401
  15.9 4.9 %collective-permute-start.5 = (bf16[2,2,8,512]{3,2,1,0:T(8,128)(2,1)S(1)}, bf16[2,2,8,512]{3,2,1,0:T(8,128)(2,1)S(1)}, u32[]{:S(2)}, u32[]{:S(2)}) collective-permute-start(bf16[2,2,8,512]{3,2,1,0:T(8,128)(2,1)S(1)} %get-tuple-element.18), channel_id=1, source_target_pairs={{0,24},{4,28},{8,16},{12,20},{16,8},{20,12},{24,0},{28,4},{1,25},{... | collective-permute-start | bytes 98312 | tf_op jit(solution)/shard_map/ppermute | solution.py:401
  18.4 4.3 %collective-permute-start.6 = (bf16[2,2,8,512]{3,2,1,0:T(8,128)(2,1)S(1)}, bf16[2,2,8,512]{3,2,1,0:T(8,128)(2,1)S(1)}, u32[]{:S(2)}, u32[]{:S(2)}) collective-permute-start(bf16[2,2,8,512]{3,2,1,0:T(8,128)(2,1)S(1)} %get-tuple-element.19), channel_id=1, source_target_pairs={{0,28},{4,24},{8,20},{12,16},{16,12},{20,8},{24,4},{28,0},{1,29},{... | collective-permute-start | bytes 98312 | tf_op jit(solution)/shard_map/ppermute | solution.py:401
  22.7 0.7 %copy-start.2 = (s32[3,512]{1,0:T(4,128)S(1)}, s32[3,512]{1,0:T(4,128)}, u32[]{:S(2)}) copy-start(s32[3,512]{1,0:T(4,128)} %cells_ref.1) | copy-start | bytes 18436
  23.4 0.7 %copy-start.4 = (s32[3,16]{1,0:T(4,128)S(1)}, s32[3,16]{1,0:T(4,128)}, u32[]{:S(2)}) copy-start(s32[3,16]{1,0:T(4,128)} %grid_ref.1) | copy-start | bytes 580
